TPU v7x, 32 devices: a whole 2x2x4 slice. The times are simulated.
32 devices in a mesh: ctx: 8 (over y, x, core), tp: 4 (over z).
Axes of the slice: x: 2, y: 2, z: 4, core: 2. Of those that a mesh axis runs over, the one named last changes fastest.
Arguments:
- tokens: bfloat16 [4096, 4096], P('ctx'), may hold values from -48 to 48
- w_query: bfloat16 [4096, 4096], P(None, 'tp'), may hold values from -0.09375 to 0.09375
- w_key: bfloat16 [4096, 4096], P(None, 'tp'), may hold values from -0.09375 to 0.09375
- w_value: bfloat16 [4096, 4096], P(None, 'tp'), may hold values from -0.09375 to 0.09375
- w_out: bfloat16 [4096, 4096], P('tp'), may hold values from -0.09375 to 0.09375
- block_doc: int32 [64], replicated, may hold values from 0 to 1, never falling along the last dimension, each value on 1 to 56 neighbouring positions
- grad_out: bfloat16 [4096, 4096], P('ctx', 'tp'), may hold values from -6 to 6
Outputs:
- output: bfloat16 [4096, 4096], P('ctx', 'tp')
- grad_tokens: bfloat16 [4096, 4096], P('ctx', 'tp')
- grad_query_weight: float32 [4096, 4096], P('ctx', 'tp')
- grad_key_weight: float32 [4096, 4096], P('ctx', 'tp')
- grad_value_weight: float32 [4096, 4096], P('ctx', 'tp')
- grad_out_weight: float32 [4096, 4096], P('tp', 'ctx')
Inputs may be any that keep to these rules, and one draw needn't show every extreme that they name: block_doc never falls along the blocks; each document covers 1 to 56 consecutive blocks.
All inputs are finite; a program needn't handle non-finite values.
Results may differ from a plain program's by a relative error of at most 0.024.
The roundings to bfloat16 on the way count: a program that leaves them out, or rounds other values in their place, can miss the bound.
Values may be sent and summed in bfloat16 or wider, within the bound.
A program may use at most 192 MiB of HBM per device.

v0:
```python
import math
import jax
import jax.numpy as jnp
from jax import lax
from jax.sharding import PartitionSpec as P

HDIM = 128
BLOCK = 64
big_negative = -1e30


def elementwise_product(pattern, left_side, right_side):
    return jnp.einsum(pattern, left_side, right_side, preferred_element_type=jnp.float32)


def attend(
    query_row_matrix,
    key_row_matrix,
    value_row_matrix,
    summary_key,
    summary_value,
    allowed,
    causal,
    score_scale_factor,
):
    near_scores = (
        elementwise_product("nqhd,nkhd->nhqk", query_row_matrix, key_row_matrix)
        * score_scale_factor
    )
    near_scores = jnp.where(causal[None, None], near_scores, big_negative)
    distant_score_matrix = (
        elementwise_product("yzxo,lxo->yzxl", query_row_matrix, summary_key) * score_scale_factor
    )
    distant_score_matrix = jnp.where(allowed[:, None, None, :], distant_score_matrix, big_negative)
    row_top = jnp.maximum(
        jnp.transpose(jnp.max(near_scores, axis=3), (0, 2, 1)),
        jnp.max(distant_score_matrix, axis=3),
    )
    near_exp = jnp.exp(near_scores - jnp.transpose(row_top, (0, 2, 1))[..., None])
    far_exp = jnp.exp(distant_score_matrix - row_top[..., None])
    denom_sum = jnp.transpose(jnp.sum(near_exp, axis=3), (0, 2, 1)) + jnp.sum(far_exp, axis=3)
    local_weight = (near_exp / jnp.transpose(denom_sum, (0, 2, 1))[..., None]).astype(jnp.bfloat16)
    distant_weight = (far_exp / denom_sum[..., None]).astype(jnp.bfloat16)
    combined_output = elementwise_product(
        "jvyb,jbvo->jyvo", local_weight, value_row_matrix
    ) + elementwise_product("gtuv,vuk->gtuk", distant_weight, summary_value)
    return (combined_output.astype(jnp.bfloat16), local_weight, distant_weight)


def attend_back(
    query_row_matrix,
    key_row_matrix,
    value_row_matrix,
    summary_key,
    summary_value,
    combined_output,
    local_weight,
    distant_weight,
    incoming_gradient,
    score_scale_factor,
):
    row_delta = jnp.sum(
        combined_output.astype(jnp.float32) * incoming_gradient.astype(jnp.float32), axis=3
    )
    near_d = elementwise_product("nqhd,nkhd->nhqk", incoming_gradient, value_row_matrix)
    distant_gradient_term = elementwise_product("yzxo,lxo->yzxl", incoming_gradient, summary_value)
    local_score_sum = (
        local_weight.astype(jnp.float32) * (near_d - jnp.transpose(row_delta, (0, 2, 1))[..., None])
    ).astype(jnp.bfloat16)
    distant_score_sum = (
        distant_weight.astype(jnp.float32) * (distant_gradient_term - row_delta[..., None])
    ).astype(jnp.bfloat16)
    query_gradient = (
        elementwise_product("jvyb,jbvo->jyvo", local_score_sum, key_row_matrix)
        + elementwise_product("gtuv,vuk->gtuk", distant_score_sum, summary_key)
    ) * score_scale_factor
    d_key = (
        elementwise_product("nhqk,nqhd->nkhd", local_score_sum, query_row_matrix)
        * score_scale_factor
    )
    d_value = elementwise_product("nhqk,nqhd->nkhd", local_weight, incoming_gradient)
    summary_key_gradient = (
        elementwise_product("agwi,agwu->iwu", distant_score_sum, query_row_matrix)
        * score_scale_factor
    )
    summary_value_gradient = elementwise_product(
        "agwi,agwu->iwu", distant_weight, incoming_gradient
    )
    return (query_gradient, d_key, d_value, summary_key_gradient, summary_value_gradient)


def back_project(grad_rows, weight):
    return lax.dot_general(
        grad_rows, weight, (((1,), (1,)), ((), ())), preferred_element_type=jnp.float32
    )


def term_maker(tokens, grad_rows):
    return lax.dot_general(
        tokens, grad_rows, (((0,), (0,)), ((), ())), preferred_element_type=jnp.float32
    )


def scatter_sum(partial, axis):
    count = lax.axis_size(axis)
    me = lax.axis_index(axis)
    width = partial.shape[1] // count

    def block(shift):
        return lax.dynamic_slice_in_dim(partial, (me + shift) % count * width, width, 1)

    total = block(0)
    for shift in range(1, count):
        ring = [(source, (source + shift) % count) for source in range(count)]
        moved = lax.ppermute(block(shift).astype(jnp.bfloat16), axis, ring)
        total = total + moved.astype(jnp.float32)
    return total


def per_device(tokens, w_query, w_key, w_value, w_out, block_doc, grad_out):
    score_scale_factor = 1.0 / math.sqrt(HDIM)
    tok_rows = tokens.shape[0]
    col_count = w_query.shape[1]
    blocks = tok_rows // BLOCK
    head_count = col_count // HDIM
    block_shape = (blocks, BLOCK, head_count, HDIM)

    def project(weight):
        return jnp.dot(tokens, weight, preferred_element_type=jnp.float32).astype(jnp.bfloat16)

    query_row_matrix = project(w_query).reshape(block_shape)
    key_row_matrix = project(w_key).reshape(block_shape)
    value_row_matrix = project(w_value).reshape(block_shape)
    own_key = key_row_matrix[:, BLOCK - 1].reshape(blocks, col_count)
    own_value = value_row_matrix[:, BLOCK - 1].reshape(blocks, col_count)
    summary = lax.all_gather(
        jnp.concatenate([own_key, own_value], axis=1), "ctx", axis=0, tiled=True
    )
    summary_key, summary_value = (summary[:, :col_count], summary[:, col_count:])
    total_blocks = summary_key.shape[0]
    summary_key = summary_key.reshape(total_blocks, head_count, HDIM)
    summary_value = summary_value.reshape(total_blocks, head_count, HDIM)
    first_block = lax.axis_index("ctx") * blocks
    query_ids = first_block + jnp.arange(blocks, dtype=jnp.int32)
    own_doc = lax.dynamic_slice_in_dim(block_doc, first_block, blocks, 0)
    block_ids = jnp.arange(total_blocks, dtype=jnp.int32)
    allowed = (block_ids[None, :] < query_ids[:, None]) & (block_doc[None, :] == own_doc[:, None])
    positions = jnp.arange(BLOCK, dtype=jnp.int32)
    causal = positions[None, :] <= positions[:, None]
    combined_output, local_weight, distant_weight = attend(
        query_row_matrix,
        key_row_matrix,
        value_row_matrix,
        summary_key,
        summary_value,
        allowed,
        causal,
        score_scale_factor,
    )
    attn = combined_output.reshape(tok_rows, col_count)
    partial_value = jnp.dot(attn, w_out, preferred_element_type=jnp.float32)
    summed = scatter_sum(partial_value, "tp")
    shard_width = summed.shape[1]
    residual = lax.dynamic_slice_in_dim(tokens, lax.axis_index("tp") * shard_width, shard_width, 1)
    output = (residual.astype(jnp.float32) + summed).astype(jnp.bfloat16)
    upstream_full = lax.all_gather(grad_out, "tp", axis=1, tiled=True)
    d_attn = back_project(upstream_full, w_out).astype(jnp.bfloat16)
    grads = attend_back(
        query_row_matrix,
        key_row_matrix,
        value_row_matrix,
        summary_key,
        summary_value,
        combined_output,
        local_weight,
        distant_weight,
        d_attn.reshape(block_shape),
        score_scale_factor,
    )
    query_gradient, d_key, d_value, summary_key_gradient, summary_value_gradient = grads
    flat_key = summary_key_gradient.reshape(total_blocks, col_count)
    flat_value = summary_value_gradient.reshape(total_blocks, col_count)
    back = lax.psum_scatter(
        jnp.concatenate([flat_key, flat_value], axis=1), "ctx", scatter_dimension=0, tiled=True
    )
    back_key, back_value = (back[:, :col_count], back[:, col_count:])
    query_gradient = query_gradient.astype(jnp.bfloat16).reshape(tok_rows, col_count)
    d_key = (
        d_key.at[:, BLOCK - 1]
        .add(back_key.reshape(blocks, head_count, HDIM))
        .astype(jnp.bfloat16)
        .reshape(tok_rows, col_count)
    )
    d_value = (
        d_value.at[:, BLOCK - 1]
        .add(back_value.reshape(blocks, head_count, HDIM))
        .astype(jnp.bfloat16)
        .reshape(tok_rows, col_count)
    )
    d_partial = (
        back_project(query_gradient, w_query)
        + back_project(d_key, w_key)
        + back_project(d_value, w_value)
    )
    d_summed = scatter_sum(d_partial, "tp")
    grad_tokens = (grad_out.astype(jnp.float32) + d_summed).astype(jnp.bfloat16)
    stacked = jnp.concatenate([query_gradient, d_key, d_value], axis=1)
    joined = lax.psum_scatter(
        term_maker(tokens, stacked).astype(jnp.bfloat16), "ctx", scatter_dimension=0, tiled=True
    ).astype(jnp.float32)
    grad_query_weight = joined[:, :col_count]
    grad_key_weight = joined[:, col_count : 2 * col_count]
    grad_value_weight = joined[:, 2 * col_count :]
    out_term = lax.dot_general(
        attn, upstream_full, (((0,), (0,)), ((), ())), preferred_element_type=jnp.float32
    )
    grad_out_weight = lax.psum_scatter(
        out_term.astype(jnp.bfloat16), "ctx", scatter_dimension=1, tiled=True
    ).astype(jnp.float32)
    return (
        output,
        grad_tokens,
        grad_query_weight,
        grad_key_weight,
        grad_value_weight,
        grad_out_weight,
    )


def solution(mesh):
    in_specs = (
        P("ctx", None),
        P(None, "tp"),
        P(None, "tp"),
        P(None, "tp"),
        P("tp", None),
        P(),
        P("ctx", "tp"),
    )
    out_specs = (
        P("ctx", "tp"),
        P("ctx", "tp"),
        P("ctx", "tp"),
        P("ctx", "tp"),
        P("ctx", "tp"),
        P("tp", "ctx"),
    )
    return jax.shard_map(
        per_device, mesh=mesh, in_specs=in_specs, out_specs=out_specs, check_vma=False
    )
```

profile of v0, /device:TPU:0, one launch (start us, length us, event | category | flops | bytes accessed | tf_op | source)
XLA Modules:
  0.0 398.2 jit_solution(12532342592921492758)
XLA Ops:
  8.0 9.3 %fusion.14 = bf16[64,8,8,128]{3,1,2,0:T(8,128)(2,1)S(1)} fusion(bf16[512,4096]{1,0:T(8,128)(2,1)} %param.11, bf16[4096,1024]{1,0:T(8,128)(2,1)} %param.12), kind=kOutput, calls=%fused_computation.41 | convolution fusion | flops 4295491584 | bytes 13631488 | tf_op jit(solution)/shard_map/dot_general | solution.py:129
  17.3 4.5 %fusion.15 = bf16[64,8,8,128]{3,1,2,0:T(8,128)(2,1)S(1)} fusion(bf16[512,4096]{1,0:T(8,128)(2,1)S(1)} %copy-done.18, bf16[4096,1024]{1,0:T(8,128)(2,1)S(1)} %copy-done.27), kind=kOutput, calls=%fused_computation.42 | convolution fusion | flops 4295491584 | bytes 13631488 | tf_op jit(solution)/shard_map/dot_general | solution.py:129
  22.3 9.5 %fusion.13 = bf16[64,8,8,128]{3,1,2,0:T(8,128)(2,1)S(1)} fusion(bf16[512,4096]{1,0:T(8,128)(2,1)} %param.11, bf16[4096,1024]{1,0:T(8,128)(2,1)} %param.14), kind=kOutput, calls=%fused_computation.40 | convolution fusion | flops 4295491584 | bytes 13631488 | tf_op jit(solution)/shard_map/dot_general | solution.py:129
  33.2 11.0 %all_gather.6 = bf16[64,2048]{1,0:T(8,128)(2,1)S(1)} all-gather(bf16[8,2048]{1,0:T(8,128)(2,1)S(1)} %pad_maximum_fusion.1), channel_id=1, replica_groups=mesh['ctx'=8,'tp'=4] {'ctx'}, dimensions={0}, use_global_device_ids=true | all-gather | bytes 294912 | tf_op jit(solution)/shard_map/all_gather | solution.py:136
  51.0 42.1 %all-gather.2.cloned.1.call-done = bf16[512,4096]{1,0:T(8,128)(2,1)} async-done(((bf16[512,1024]{1,0:T(8,128)(2,1)}), bf16[512,4096]{1,0:T(8,128)(2,1)}) %all-gather.2.cloned.1.call-update) | async-done | bytes 4194320 | tf_op jit(solution)/shard_map/all_gather | solution.py:166
  93.0 9.2 %fusion.16 = bf16[64,8,8,128]{3,1,2,0:T(8,128)(2,1)S(1)} fusion(bf16[512,4096]{1,0:T(8,128)(2,1)} %all-gather.2.cloned.1.call-done, bf16[1024,4096]{1,0:T(8,128)(2,1)} %param.15), kind=kOutput, calls=%fused_computation.43 | convolution fusion | flops 4295491584 | bytes 13631488 | tf_op jit(solution)/shard_map/dot_general | solution.py:93
  110.4 9.0 %convolution_convert_fusion = bf16[1024,4096]{1,0:T(8,128)(2,1)} fusion(bf16[512,4096]{1,0:T(8,128)(2,1)} %all-gather.2.cloned.1.call-done, bf16[64,8,8,128]{3,2,1,0:T(8,128)(2,1)S(1)} %bitcast.187), kind=kOutput, calls=%fused_computation.2 | convolution fusion | flops 4299161600 | bytes 13631488 | tf_op jit(solution)/shard_map/dot_general | solution.py:214
  130.2 12.8 %reduce-scatter.4.cloned.1.call-done = f32[8,2048]{1,0:T(8,128)} async-done(((f32[64,2048]{1,0:T(8,128)}), f32[8,2048]{1,0:T(8,128)}) %reduce-scatter.4.cloned.1.call-update) | async-done | bytes 65552 | tf_op jit(solution)/shard_map/reduce_scatter | solution.py:183
  153.6 18.3 %convert_bitcast_fusion = bf16[4096,3072]{0,1:T(8,128)(2,1)} fusion(bf16[512,4096]{1,0:T(8,128)(2,1)S(1)} %copy-done.19, bf16[512,1024]{1,0:T(8,128)(2,1)S(1)} %bitcast.191, bf16[512,1024]{1,0:T(8,128)(2,1)S(1)} %bitcast.190, bf16[512,1024]{1,0:T(8,128)(2,1)S(1)} %bitcast.189), kind=kOutput, calls=%fused_computation | convolution fusion | flops 12906921984 | bytes 32505856 | tf_op jit(solution)/shard_map/dot_general | solution.py:99
  173.3 10.1 %fusion.20 = f32[512,4096]{1,0:T(8,128)} fusion(bf16[1024,4096]{1,0:T(8,128)(2,1)} %param.15, bf16[64,8,8,128]{3,2,1,0:T(8,128)(2,1)S(1)} %bitcast.188), kind=kOutput, calls=%fused_computation.52 | convolution fusion | flops 4294967296 | bytes 17825792 | tf_op jit(solution)/shard_map/dot_general | solution.py:161
  183.3 5.0 %dynamic-slice_convert_fusion.5 = (bf16[512,1024]{1,0:T(8,128)(2,1)}, bf16[512,1024]{1,0:T(8,128)(2,1)}, bf16[512,1024]{1,0:T(8,128)(2,1)}) fusion(f32[512,4096]{1,0:T(8,128)} %fusion.20, s32[]{:T(128)S(6)} %select_n.64, s32[]{:T(128)S(6)} %select_n.68, s32[]{:T(128)S(6)} %select_n.66), kind=kLoop, calls=%fused_computation.27 | loop fusion | bytes 6291468 | tf_op jit(solution)/shard_map/convert_element_type | solution.py:115
  192.8 10.5 %fusion.48 = f32[512,4096]{1,0:T(8,128)} fusion(bf16[4096,1024]{1,0:T(8,128)(2,1)} %param.12, bf16[64,8,8,128]{3,2,1,0:T(8,128)(2,1)S(1)} %bitcast.178), kind=kOutput, calls=%fused_computation.104 | convolution fusion | flops 4294967296 | bytes 17825792 | tf_op jit(solution)/shard_map/dot_general | solution.py:93
  203.3 6.8 %fusion.49 = f32[512,4096]{1,0:T(8,128)} fusion(bf16[4096,1024]{1,0:T(8,128)(2,1)S(1)} %bitcast.200, bf16[64,8,8,128]{3,2,1,0:T(8,128)(2,1)S(1)} %bitcast.182), kind=kOutput, calls=%fused_computation.105 | convolution fusion | flops 4294967296 | bytes 17825792 | tf_op jit(solution)/shard_map/dot_general | solution.py:93
  210.1 12.9 %add_add_fusion = f32[512,4096]{1,0:T(8,128)} fusion(f32[512,4096]{1,0:T(8,128)} %fusion.48, f32[512,4096]{1,0:T(8,128)} %fusion.49, bf16[4096,1024]{1,0:T(8,128)(2,1)} %param.14, bf16[64,8,8,128]{3,2,1,0:T(8,128)(2,1)S(1)} %bitcast.180), kind=kOutput, calls=%fused_computation.1 | convolution fusion | flops 4299161600 | bytes 34603008 | tf_op jit(solution)/shard_map/dot_general | solution.py:93
  223.0 4.3 %dynamic-slice_convert_fusion.2 = (bf16[512,1024]{1,0:T(8,128)(2,1)}, bf16[512,1024]{1,0:T(8,128)(2,1)S(1)}, bf16[512,1024]{1,0:T(8,128)(2,1)S(1)}) fusion(f32[512,4096]{1,0:T(8,128)} %add_add_fusion, s32[]{:T(128)S(6)} %select_n.64, s32[]{:T(128)S(6)} %select_n.68, s32[]{:T(128)S(6)} %select_n.66), kind=kLoop, calls=%fused_computation.20 | loop fusion | bytes 6291468 | tf_op jit(solution)/shard_map/convert_element_type | solution.py:115
  231.2 30.6 %collective-permute-start.4 = (bf16[512,1024]{1,0:T(8,128)(2,1)S(1)}, bf16[512,1024]{1,0:T(8,128)(2,1)}, u32[]{:S(2)}, u32[]{:S(2)}) collective-permute-start(bf16[512,1024]{1,0:T(8,128)(2,1)S(1)} %get-tuple-element.56), channel_id=1, source_target_pairs={{0,2},{1,3},{2,0},{3,1},{4,6},{5,7},{6,4},{7,5},{8,10},{9,11},{10,... | collective-permute-start | bytes 3145736 | tf_op jit(solution)/shard_map/ppermute | solution.py:115
  261.8 44.6 %collective-permute-done.1 = bf16[512,1024]{1,0:T(8,128)(2,1)} collective-permute-done((bf16[512,1024]{1,0:T(8,128)(2,1)}, bf16[512,1024]{1,0:T(8,128)(2,1)}, u32[]{:S(2)}, u32[]{:S(2)}) %collective-permute-start.1) | collective-permute-done | bytes 1048608 | tf_op jit(solution)/shard_map/ppermute | solution.py:115
  306.4 4.8 %add_convert_fusion.1 = bf16[512,1024]{1,0:T(8,128)(2,1)} fusion(bf16[512,1024]{1,0:T(8,128)(2,1)} %collective-permute-done.2, bf16[512,1024]{1,0:T(8,128)(2,1)} %collective-permute-done.1, bf16[512,1024]{1,0:T(8,128)(2,1)} %collective-permute-done, f32[512,4096]{1,0:T(8,128)} %fusion.20, s32[]{:T(128)S(6)} %select_n.62, bf16[512,4096]{1,0:T(8,128)(2,1)} %param.11, ...), kind=kLoop, calls=%fused_computation.24 | loop fusion | flops 4718592 | bytes 7340040 | tf_op jit(solution)/shard_map/convert_element_type | solution.py:165
  311.2 60.4 %collective-permute-done.4 = bf16[512,1024]{1,0:T(8,128)(2,1)} collective-permute-done((bf16[512,1024]{1,0:T(8,128)(2,1)S(1)}, bf16[512,1024]{1,0:T(8,128)(2,1)}, u32[]{:S(2)}, u32[]{:S(2)}) %collective-permute-start.4) | collective-permute-done | bytes 1048608 | tf_op jit(solution)/shard_map/ppermute | solution.py:115
  371.6 4.7 %add_convert_fusion = bf16[512,1024]{1,0:T(8,128)(2,1)} fusion(bf16[512,1024]{1,0:T(8,128)(2,1)} %collective-permute-done.5, bf16[512,1024]{1,0:T(8,128)(2,1)} %collective-permute-done.4, bf16[512,1024]{1,0:T(8,128)(2,1)} %collective-permute-done.3, f32[512,4096]{1,0:T(8,128)} %add_add_fusion, s32[]{:T(128)S(6)} %select_n.62, bf16[512,1024]{1,0:T(8,128)(2,1)S(1)} %copy-done.7), kind=kLoop, calls=%fused_computation.17 | loop fusion | flops 4718592 | bytes 7340036 | tf_op jit(solution)/shard_map/convert_element_type | solution.py:206
  376.3 2.9 convert_element_type.147
  379.2 4.8 %fusion.50 = (f32[512,1024]{0,1:T(8,128)}, f32[512,1024]{0,1:T(8,128)}, f32[512,1024]{0,1:T(8,128)S(1)}) fusion(bf16[512,3072]{0,1:T(8,128)(2,1)} %reduce-scatter.6.cloned.1.call-done), kind=kLoop, calls=%fused_computation.106 | loop fusion | bytes 12582912 | tf_op jit(solution)/shard_map/slice | solution.py:213
  383.9 2.9 copy.147
  386.8 2.9 copy.146
  (137 shorter events, 50.0 us)
Async XLA Ops:
  7.2 85.9 %all-gather.2.cloned.1.call-start = ((), (), s32[]{:S(2)}) async-start(), calls=%async_computation.3 | async-start | bytes 5242880 | tf_op jit(solution)/shard_map/all_gather | solution.py:166
  7.9 135.1 %reduce-scatter.4.cloned.1.call-start = ((), (), s32[]{:S(2)}) async-start(), calls=%async_computation.4 | async-start | bytes 589824 | tf_op jit(solution)/shard_map/reduce_scatter | solution.py:183
  7.9 9.3 %copy-start.18 = (bf16[512,4096]{1,0:T(8,128)(2,1)S(1)}, bf16[512,4096]{1,0:T(8,128)(2,1)}, u32[]{:S(2)}) copy-start(bf16[512,4096]{1,0:T(8,128)(2,1)} %param.11) | copy-start | bytes 12582916
  8.0 9.3 %copy-start.27 = (bf16[4096,1024]{1,0:T(8,128)(2,1)S(1)}, bf16[4096,1024]{1,0:T(8,128)(2,1)}, u32[]{:S(2)}) copy-start(bf16[4096,1024]{1,0:T(8,128)(2,1)} %param.13) | copy-start | bytes 25165828
  22.3 23.3 %copy-start = (bf16[64,8,8,128]{3,2,1,0:T(8,128)(2,1)}, bf16[64,8,8,128]{3,2,1,0:T(8,128)(2,1)S(1)}, u32[]{:S(2)}) copy-start(bf16[64,8,8,128]{3,2,1,0:T(8,128)(2,1)S(1)} %copy.169) | copy-start | bytes 3145732
  31.9 12.4 %copy-start.26 = (s32[64]{0:T(128)S(1)}, s32[64]{0:T(128)}, u32[]{:S(2)}) copy-start(s32[64]{0:T(128)} %param.16) | copy-start | bytes 772
  104.9 2.8 copy-start.22
  110.3 266.0 %reduce-scatter.8.cloned.1.call-start = ((), (), s32[]{:S(2)}) async-start(), calls=%async_computation.6 | async-start | bytes 9437184 | tf_op jit(solution)/shard_map/reduce_scatter | solution.py:217
  119.4 4.5 %copy-start.14 = (bf16[64,8,8,128]{3,2,1,0:T(8,128)(2,1)S(1)}, bf16[64,8,8,128]{3,2,1,0:T(8,128)(2,1)}, u32[]{:S(2)}) copy-start(bf16[64,8,8,128]{3,2,1,0:T(8,128)(2,1)} %copy-done.12) | copy-start | bytes 3145732
  119.4 4.5 %copy-start.23 = (f32[8,64,8]{1,2,0:T(8,128)S(1)}, f32[8,64,8]{1,2,0:T(8,128)}, u32[]{:S(2)}) copy-start(f32[8,64,8]{1,2,0:T(8,128)} %copy-done.22) | copy-start | bytes 49156
  119.4 259.8 %reduce-scatter.6.cloned.1.call-start = ((), (), s32[]{:S(2)}) async-start(), calls=%async_computation.5 | async-start | bytes 28311552 | tf_op jit(solution)/shard_map/reduce_scatter | solution.py:208
  120.1 3.8 copy-start.10
  150.0 3.1 copy-start.19
  150.7 2.9 copy-start.17
  183.3 9.5 %copy-start.3 = (bf16[8,64,8,128]{3,2,1,0:T(8,128)(2,1)S(1)}, bf16[8,64,8,128]{3,2,1,0:T(8,128)(2,1)}, u32[]{:S(2)}) copy-start(bf16[8,64,8,128]{3,2,1,0:T(8,128)(2,1)} %copy-done.2) | copy-start | bytes 3145732
  188.3 42.9 %collective-permute-start = (bf16[512,1024]{1,0:T(8,128)(2,1)}, bf16[512,1024]{1,0:T(8,128)(2,1)}, u32[]{:S(2)}, u32[]{:S(2)}) collective-permute-start(bf16[512,1024]{1,0:T(8,128)(2,1)} %get-tuple-element.57), channel_id=1, source_target_pairs={{0,1},{1,2},{2,3},{3,0},{4,5},{5,6},{6,7},{7,4},{8,9},{9,10},{10,1... | collective-permute-start | bytes 3145736 | tf_op jit(solution)/shard_map/ppermute | solution.py:115
  189.7 72.1 %collective-permute-start.2 = (bf16[512,1024]{1,0:T(8,128)(2,1)}, bf16[512,1024]{1,0:T(8,128)(2,1)}, u32[]{:S(2)}, u32[]{:S(2)}) collective-permute-start(bf16[512,1024]{1,0:T(8,128)(2,1)} %get-tuple-element.58), channel_id=1, source_target_pairs={{0,3},{1,0},{2,1},{3,2},{4,7},{5,4},{6,5},{7,6},{8,11},{9,8},{10,9... | collective-permute-start | bytes 3145736 | tf_op jit(solution)/shard_map/ppermute | solution.py:115
  192.3 11.0 %slice-start = ((s8[8388608]{0:T(1024)(128)(4,1)}), s8[4194304]{0:T(1024)(128)(4,1)S(1)}, s32[]{:S(2)}) async-start(s8[8388608]{0:T(1024)(128)(4,1)} %bitcast.199), calls=%async_computation.7 | async-start | bytes 8388608
  192.3 11.0 %slice-start.1 = ((s8[8388608]{0:T(1024)(128)(4,1)}), s8[4194304]{0:T(1024)(128)(4,1)S(1)}, s32[]{:S(2)}) async-start(s8[8388608]{0:T(1024)(128)(4,1)} %bitcast.199), calls=%async_computation.8 | async-start | bytes 8388608
  192.3 114.1 %collective-permute-start.1 = (bf16[512,1024]{1,0:T(8,128)(2,1)}, bf16[512,1024]{1,0:T(8,128)(2,1)}, u32[]{:S(2)}, u32[]{:S(2)}) collective-permute-start(bf16[512,1024]{1,0:T(8,128)(2,1)} %get-tuple-element.59), channel_id=1, source_target_pairs={{0,2},{1,3},{2,0},{3,1},{4,6},{5,7},{6,4},{7,5},{8,10},{9,11},{10,... | collective-permute-start | bytes 3145736 | tf_op jit(solution)/shard_map/ppermute | solution.py:115
  227.4 83.8 %collective-permute-start.3 = (bf16[512,1024]{1,0:T(8,128)(2,1)}, bf16[512,1024]{1,0:T(8,128)(2,1)}, u32[]{:S(2)}, u32[]{:S(2)}) collective-permute-start(bf16[512,1024]{1,0:T(8,128)(2,1)} %get-tuple-element.54), channel_id=1, source_target_pairs={{0,1},{1,2},{2,3},{3,0},{4,5},{5,6},{6,7},{7,4},{8,9},{9,10},{10,1... | collective-permute-start | bytes 3145736 | tf_op jit(solution)/shard_map/ppermute | solution.py:115
  228.7 82.5 %collective-permute-start.5 = (bf16[512,1024]{1,0:T(8,128)(2,1)S(1)}, bf16[512,1024]{1,0:T(8,128)(2,1)}, u32[]{:S(2)}, u32[]{:S(2)}) collective-permute-start(bf16[512,1024]{1,0:T(8,128)(2,1)S(1)} %get-tuple-element.55), channel_id=1, source_target_pairs={{0,3},{1,0},{2,1},{3,2},{4,7},{5,4},{6,5},{7,6},{8,11},{9,8},{10,9... | collective-permute-start | bytes 3145736 | tf_op jit(solution)/shard_map/ppermute | solution.py:115
  231.2 140.4 %collective-permute-start.4 = (bf16[512,1024]{1,0:T(8,128)(2,1)S(1)}, bf16[512,1024]{1,0:T(8,128)(2,1)}, u32[]{:S(2)}, u32[]{:S(2)}) collective-permute-start(bf16[512,1024]{1,0:T(8,128)(2,1)S(1)} %get-tuple-element.56), channel_id=1, source_target_pairs={{0,2},{1,3},{2,0},{3,1},{4,6},{5,7},{6,4},{7,5},{8,10},{9,11},{10,... | collective-permute-start | bytes 3145736 | tf_op jit(solution)/shard_map/ppermute | solution.py:115
  261.8 109.8 %copy-start.7 = (bf16[512,1024]{1,0:T(8,128)(2,1)S(1)}, bf16[512,1024]{1,0:T(8,128)(2,1)}, u32[]{:S(2)}) copy-start(bf16[512,1024]{1,0:T(8,128)(2,1)} %param.17) | copy-start | bytes 3145732
  (16 other events, 19.0 us)
Sparse Core Ops, SparseCore 0:
  9.5 83.4 all-gather.1
  110.4 32.5 reduce-scatter.3
  146.5 71.3 reduce-scatter.7
  221.3 155.9 reduce-scatter.5
where the time goes:
time: 406 us; the launch traced here: 398 us
  waiting for transfers between devices  161 us (40%)
  matrix products  112 us (28%)
  local copies, waits for them, and re-layouts  43.7 us (11%)
  starting transfers between devices  39.1 us (10%)
  other arithmetic  17.1 us (4%)
  between operations  14.6 us (4%)
  blocking collectives  11 us (3%)
    ppermute x6, waiting for transfers between devices, scatter_sum(): moved = lax.ppermute(block(shift).astype(jnp.bfloat16), axis, ring)  105 us
    all_gather x1, waiting for transfers between devices, per_device(): upstream_full = lax.all_gather(grad_out, 'tp', axis=1, tiled=True)  42.1 us
    dot_general x4, matrix products, back_project(): lax.dot_general(grad_rows, weight, (((1,), (1,)), ((), ())), preferred_el...  39.4 us
    ppermute x6, starting transfers between devices, scatter_sum(): moved = lax.ppermute(block(shift).astype(jnp.bfloat16), axis, ring)  39 us
    dot_general x3, matrix products, project(): jnp.dot(tokens, weight, preferred_element_type=jnp.float32)  23.3 us
    unnamed x76, local copies, waits for them, and re-layouts  22.3 us
    dot_general x1, matrix products, term_maker(): lax.dot_general(tokens, grad_rows, (((0,), (0,)), ((), ())), preferred_el...  18.3 us
    reduce_scatter x1, waiting for transfers between devices, per_device(): lax.psum_scatter(jnp.concatenate([flat_key, flat_value], axis=1), 'ctx',...  12.8 us
  transfers between devices with their start and end apart: 10, of which 4 were waited for; matrix products, arithmetic and copies ran while one was open for 34% of the time, Pallas kernels for 0%

commit v1 on v0

--- a/solution.py
+++ b/solution.py
@@ -163,7 +163,10 @@
     shard_width = summed.shape[1]
     residual = lax.dynamic_slice_in_dim(tokens, lax.axis_index("tp") * shard_width, shard_width, 1)
     output = (residual.astype(jnp.float32) + summed).astype(jnp.bfloat16)
-    upstream_full = lax.all_gather(grad_out, "tp", axis=1, tiled=True)
+    devices = lax.axis_size("tp")
+    pieces = jnp.stack([grad_out for _ in range(devices)])
+    pieces = lax.all_to_all(pieces, "tp", split_axis=0, concat_axis=0)
+    upstream_full = jnp.concatenate(pieces, axis=1)
     d_attn = back_project(upstream_full, w_out).astype(jnp.bfloat16)
     grads = attend_back(
         query_row_matrix,

time: 406 us -> 423 us (1.042)
  waiting for transfers between devices: 161 us -> 169 us
  starting transfers between devices: 39.1 us -> 45.4 us
    all_to_all x0 -> x1, waiting for transfers between devices: none -> 49.4 us  [per_device(): pieces = lax.all_to_all(pieces, 'tp', split_axis=0, concat_axis=0)]
    all_gather x1 -> x0, waiting for transfers between devices: 42.1 us -> none  [per_device(): upstream_full = lax.all_gather(grad_out, 'tp', axis=1, tiled=True)]
    all_to_all x0 -> x1, starting transfers between devices: none -> 6.35 us  [per_device(): pieces = lax.all_to_all(pieces, 'tp', split_axis=0, concat_axis=0)]
    unnamed x76 -> x73, local copies, waits for them, and re-layouts: 22.3 us -> 25.4 us
  transfers between devices with their start and end apart: 10 -> 10, of which waited for: 4 -> 5; matrix products, arithmetic and copies ran while one was open for 34% -> 32% of each run, Pallas kernels for 0% -> 0%
where the time goes in v1:
time: 423 us; the launch traced here: 415 us
  waiting for transfers between devices  169 us (40%)
  matrix products  114 us (27%)
  starting transfers between devices  45.4 us (11%)
  local copies, waits for them, and re-layouts  45.2 us (11%)
  other arithmetic  16.9 us (4%)
  between operations  14.5 us (3%)
  blocking collectives  9.52 us (2%)
    ppermute x6, waiting for transfers between devices, scatter_sum(): moved = lax.ppermute(block(shift).astype(jnp.bfloat16), axis, ring)  105 us
    all_to_all x1, waiting for transfers between devices, per_device(): pieces = lax.all_to_all(pieces, 'tp', split_axis=0, concat_axis=0)  49.4 us
    dot_general x4, matrix products, back_project(): lax.dot_general(grad_rows, weight, (((1,), (1,)), ((), ())), preferred_el...  39.5 us
    ppermute x6, starting transfers between devices, scatter_sum(): moved = lax.ppermute(block(shift).astype(jnp.bfloat16), axis, ring)  39 us
    dot_general x3, matrix products, project(): jnp.dot(tokens, weight, preferred_element_type=jnp.float32)  25.8 us
    unnamed x73, local copies, waits for them, and re-layouts  25.4 us
    dot_general x1, matrix products, term_maker(): lax.dot_general(tokens, grad_rows, (((0,), (0,)), ((), ())), preferred_el...  20.8 us
    reduce_scatter x1, waiting for transfers between devices, per_device(): lax.psum_scatter(jnp.concatenate([flat_key, flat_value], axis=1), 'ctx',...  13.5 us
  transfers between devices with their start and end apart: 10, of which 5 were waited for; matrix products, arithmetic and copies ran while one was open for 32% of the time, Pallas kernels for 0%

profile of v1, /device:TPU:0, one launch (start us, length us, event | category | flops | bytes accessed | tf_op | source)
XLA Modules:
  0.0 415.0 jit_solution(16406412908146203911)
XLA Ops:
  11.0 6.3 %all-to-all-start = ((bf16[4,512,1024]{1,2,0:T(8,128)(2,1)}), bf16[4,512,1024]{1,2,0:T(8,128)(2,1)}, u32[]{:S(2)}, u32[]{:S(2)}) async-start(bf16[4,512,1024]{1,2,0:T(8,128)(2,1)} %stack.2), calls=%async_computation | async-start | bytes 8388608 | tf_op jit(solution)/shard_map/all_to_all | solution.py:168
  17.4 9.3 %fusion.14 = bf16[64,8,8,128]{3,1,2,0:T(8,128)(2,1)S(1)} fusion(bf16[512,4096]{1,0:T(8,128)(2,1)} %param.11, bf16[4096,1024]{1,0:T(8,128)(2,1)} %param.12), kind=kOutput, calls=%fused_computation.41 | convolution fusion | flops 4295491584 | bytes 13631488 | tf_op jit(solution)/shard_map/dot_general | solution.py:129
  26.7 7.0 %fusion.15 = bf16[64,8,8,128]{3,1,2,0:T(8,128)(2,1)S(1)} fusion(bf16[512,4096]{1,0:T(8,128)(2,1)S(1)} %copy-done.18, bf16[4096,1024]{1,0:T(8,128)(2,1)} %param.13), kind=kOutput, calls=%fused_computation.42 | convolution fusion | flops 4295491584 | bytes 13631488 | tf_op jit(solution)/shard_map/dot_general | solution.py:129
  34.3 9.5 %fusion.13 = bf16[64,8,8,128]{3,1,2,0:T(8,128)(2,1)S(1)} fusion(bf16[512,4096]{1,0:T(8,128)(2,1)} %param.11, bf16[4096,1024]{1,0:T(8,128)(2,1)} %param.14), kind=kOutput, calls=%fused_computation.40 | convolution fusion | flops 4295491584 | bytes 13631488 | tf_op jit(solution)/shard_map/dot_general | solution.py:129
  45.1 9.5 %all_gather.3 = bf16[64,2048]{1,0:T(8,128)(2,1)S(1)} all-gather(bf16[8,2048]{1,0:T(8,128)(2,1)S(1)} %pad_maximum_fusion.1), channel_id=1, replica_groups=mesh['ctx'=8,'tp'=4] {'ctx'}, dimensions={0}, use_global_device_ids=true | all-gather | bytes 294912 | tf_op jit(solution)/shard_map/all_gather | solution.py:136
  61.4 49.4 %all-to-all-done = bf16[4,512,1024]{1,2,0:T(8,128)(2,1)} async-done(((bf16[4,512,1024]{1,2,0:T(8,128)(2,1)}), bf16[4,512,1024]{1,2,0:T(8,128)(2,1)}, u32[]{:S(2)}, u32[]{:S(2)}) %all-to-all-start) | async-done | bytes 4194336 | tf_op jit(solution)/shard_map/all_to_all | solution.py:168
  110.8 9.2 %fusion.16 = bf16[64,8,8,128]{3,1,2,0:T(8,128)(2,1)S(1)} fusion(bf16[512,4096]{0,1:T(8,128)(2,1)} %bitcast.10, bf16[1024,4096]{1,0:T(8,128)(2,1)} %param.15), kind=kOutput, calls=%fused_computation.43 | convolution fusion | flops 4295491584 | bytes 13631488 | tf_op jit(solution)/shard_map/dot_general | solution.py:93
  128.2 9.0 %convolution_convert_fusion = bf16[1024,4096]{1,0:T(8,128)(2,1)} fusion(bf16[512,4096]{0,1:T(8,128)(2,1)} %bitcast.10, bf16[64,8,8,128]{3,2,1,0:T(8,128)(2,1)S(1)} %bitcast.190), kind=kOutput, calls=%fused_computation.2 | convolution fusion | flops 4299161600 | bytes 13631488 | tf_op jit(solution)/shard_map/dot_general | solution.py:217
  148.1 13.5 %reduce-scatter.4.cloned.1.call-done = f32[8,2048]{1,0:T(8,128)} async-done(((f32[64,2048]{1,0:T(8,128)}), f32[8,2048]{1,0:T(8,128)}) %reduce-scatter.4.cloned.1.call-update) | async-done | bytes 65552 | tf_op jit(solution)/shard_map/reduce_scatter | solution.py:186
  169.4 20.8 %convert_bitcast_fusion = bf16[4096,3072]{0,1:T(8,128)(2,1)} fusion(bf16[512,4096]{1,0:T(8,128)(2,1)} %param.11, bf16[512,1024]{1,0:T(8,128)(2,1)S(1)} %bitcast.194, bf16[512,1024]{1,0:T(8,128)(2,1)S(1)} %bitcast.193, bf16[512,1024]{1,0:T(8,128)(2,1)S(1)} %bitcast.192), kind=kOutput, calls=%fused_computation | convolution fusion | flops 12906921984 | bytes 32505856 | tf_op jit(solution)/shard_map/dot_general | solution.py:99
  191.6 6.9 %fusion.20 = f32[512,4096]{1,0:T(8,128)S(1)} fusion(bf16[1024,4096]{1,0:T(8,128)(2,1)} %param.15, bf16[64,8,8,128]{3,2,1,0:T(8,128)(2,1)S(1)} %bitcast.191), kind=kOutput, calls=%fused_computation.52 | convolution fusion | flops 4294967296 | bytes 17825792 | tf_op jit(solution)/shard_map/dot_general | solution.py:161
  198.5 3.2 copy-done.7
  208.3 10.6 %fusion.48 = f32[512,4096]{1,0:T(8,128)} fusion(bf16[4096,1024]{1,0:T(8,128)(2,1)} %param.12, bf16[64,8,8,128]{3,2,1,0:T(8,128)(2,1)S(1)} %bitcast.181), kind=kOutput, calls=%fused_computation.104 | convolution fusion | flops 4294967296 | bytes 17825792 | tf_op jit(solution)/shard_map/dot_general | solution.py:93
  218.9 6.8 %fusion.49 = f32[512,4096]{1,0:T(8,128)} fusion(bf16[4096,1024]{1,0:T(8,128)(2,1)S(1)} %bitcast.203, bf16[64,8,8,128]{3,2,1,0:T(8,128)(2,1)S(1)} %bitcast.185), kind=kOutput, calls=%fused_computation.105 | convolution fusion | flops 4294967296 | bytes 17825792 | tf_op jit(solution)/shard_map/dot_general | solution.py:93
  225.7 12.9 %add_add_fusion = f32[512,4096]{1,0:T(8,128)} fusion(f32[512,4096]{1,0:T(8,128)} %fusion.48, f32[512,4096]{1,0:T(8,128)} %fusion.49, bf16[4096,1024]{1,0:T(8,128)(2,1)} %param.14, bf16[64,8,8,128]{3,2,1,0:T(8,128)(2,1)S(1)} %bitcast.183), kind=kOutput, calls=%fused_computation.1 | convolution fusion | flops 4299161600 | bytes 34603008 | tf_op jit(solution)/shard_map/dot_general | solution.py:93
  238.6 4.3 %dynamic-slice_convert_fusion.2 = (bf16[512,1024]{1,0:T(8,128)(2,1)}, bf16[512,1024]{1,0:T(8,128)(2,1)S(1)}, bf16[512,1024]{1,0:T(8,128)(2,1)S(1)}) fusion(f32[512,4096]{1,0:T(8,128)} %add_add_fusion, s32[]{:T(128)S(6)} %select_n.64, s32[]{:T(128)S(6)} %select_n.68, s32[]{:T(128)S(6)} %select_n.66), kind=kLoop, calls=%fused_computation.20 | loop fusion | bytes 6291468 | tf_op jit(solution)/shard_map/convert_element_type | solution.py:115
  246.7 30.5 %collective-permute-start.4 = (bf16[512,1024]{1,0:T(8,128)(2,1)S(1)}, bf16[512,1024]{1,0:T(8,128)(2,1)}, u32[]{:S(2)}, u32[]{:S(2)}) collective-permute-start(bf16[512,1024]{1,0:T(8,128)(2,1)S(1)} %get-tuple-element.56), channel_id=1, source_target_pairs={{0,2},{1,3},{2,0},{3,1},{4,6},{5,7},{6,4},{7,5},{8,10},{9,11},{10,... | collective-permute-start | bytes 3145736 | tf_op jit(solution)/shard_map/ppermute | solution.py:115
  277.2 44.5 %collective-permute-done.1 = bf16[512,1024]{1,0:T(8,128)(2,1)} collective-permute-done((bf16[512,1024]{1,0:T(8,128)(2,1)}, bf16[512,1024]{1,0:T(8,128)(2,1)}, u32[]{:S(2)}, u32[]{:S(2)}) %collective-permute-start.1) | collective-permute-done | bytes 1048608 | tf_op jit(solution)/shard_map/ppermute | solution.py:115
  321.7 4.7 %add_convert_fusion.1 = bf16[512,1024]{1,0:T(8,128)(2,1)} fusion(bf16[512,1024]{1,0:T(8,128)(2,1)} %collective-permute-done.2, bf16[512,1024]{1,0:T(8,128)(2,1)} %collective-permute-done.1, bf16[512,1024]{1,0:T(8,128)(2,1)S(1)} %collective-permute-done, f32[512,4096]{1,0:T(8,128)} %copy-done.7, s32[]{:T(128)S(6)} %select_n.62, bf16[512,4096]{1,0:T(8,128)(2,1)} %param.11, ...), kind=kLoop, calls=%fused_computation.24 | loop fusion | flops 4718592 | bytes 7340040 | tf_op jit(solution)/shard_map/convert_element_type | solution.py:165
  326.4 60.5 %collective-permute-done.4 = bf16[512,1024]{1,0:T(8,128)(2,1)} collective-permute-done((bf16[512,1024]{1,0:T(8,128)(2,1)S(1)}, bf16[512,1024]{1,0:T(8,128)(2,1)}, u32[]{:S(2)}, u32[]{:S(2)}) %collective-permute-start.4) | collective-permute-done | bytes 1048608 | tf_op jit(solution)/shard_map/ppermute | solution.py:115
  386.9 4.6 %add_convert_fusion = bf16[512,1024]{1,0:T(8,128)(2,1)} fusion(bf16[512,1024]{1,0:T(8,128)(2,1)} %collective-permute-done.5, bf16[512,1024]{1,0:T(8,128)(2,1)} %collective-permute-done.4, bf16[512,1024]{1,0:T(8,128)(2,1)} %collective-permute-done.3, f32[512,4096]{1,0:T(8,128)} %add_add_fusion, s32[]{:T(128)S(6)} %select_n.62, bf16[512,1024]{1,0:T(8,128)(2,1)S(1)} %copy-done.6), kind=kLoop, calls=%fused_computation.17 | loop fusion | flops 4718592 | bytes 7340036 | tf_op jit(solution)/shard_map/convert_element_type | solution.py:209
  395.9 4.8 %fusion.50 = (f32[512,1024]{0,1:T(8,128)}, f32[512,1024]{0,1:T(8,128)}, f32[512,1024]{0,1:T(8,128)S(1)}) fusion(bf16[512,3072]{0,1:T(8,128)(2,1)} %reduce-scatter.6.cloned.1.call-done), kind=kLoop, calls=%fused_computation.106 | loop fusion | bytes 12582912 | tf_op jit(solution)/shard_map/slice | solution.py:216
  400.7 2.9 copy.150
  403.6 2.9 copy.149
  (134 shorter events, 56.9 us)
Async XLA Ops:
  11.0 99.8 %all-to-all-start = ((bf16[4,512,1024]{1,2,0:T(8,128)(2,1)}), bf16[4,512,1024]{1,2,0:T(8,128)(2,1)}, u32[]{:S(2)}, u32[]{:S(2)}) async-start(bf16[4,512,1024]{1,2,0:T(8,128)(2,1)} %stack.2), calls=%async_computation | async-start | bytes 8388608 | tf_op jit(solution)/shard_map/all_to_all | solution.py:168
  17.4 144.1 %reduce-scatter.4.cloned.1.call-start = ((), (), s32[]{:S(2)}) async-start(), calls=%async_computation.4 | async-start | bytes 589824 | tf_op jit(solution)/shard_map/reduce_scatter | solution.py:186
  17.4 9.3 %copy-start.18 = (bf16[512,4096]{1,0:T(8,128)(2,1)S(1)}, bf16[512,4096]{1,0:T(8,128)(2,1)}, u32[]{:S(2)}) copy-start(bf16[512,4096]{1,0:T(8,128)(2,1)} %param.11) | copy-start | bytes 12582916
  34.3 21.9 %copy-start = (bf16[64,8,8,128]{3,2,1,0:T(8,128)(2,1)}, bf16[64,8,8,128]{3,2,1,0:T(8,128)(2,1)S(1)}, u32[]{:S(2)}) copy-start(bf16[64,8,8,128]{3,2,1,0:T(8,128)(2,1)S(1)} %copy.172) | copy-start | bytes 3145732
  43.8 11.0 %copy-start.25 = (s32[64]{0:T(128)S(1)}, s32[64]{0:T(128)}, u32[]{:S(2)}) copy-start(s32[64]{0:T(128)} %param.16) | copy-start | bytes 772
  56.8 1.9 copy-start.9
  120.0 1.6 copy-start.11
  122.7 3.1 copy-start.21
  128.1 263.4 %reduce-scatter.8.cloned.1.call-start = ((), (), s32[]{:S(2)}) async-start(), calls=%async_computation.6 | async-start | bytes 9437184 | tf_op jit(solution)/shard_map/reduce_scatter | solution.py:220
  137.2 4.5 %copy-start.14 = (bf16[64,8,8,128]{3,2,1,0:T(8,128)(2,1)S(1)}, bf16[64,8,8,128]{3,2,1,0:T(8,128)(2,1)}, u32[]{:S(2)}) copy-start(bf16[64,8,8,128]{3,2,1,0:T(8,128)(2,1)} %copy-done.12) | copy-start | bytes 3145732
  137.2 4.5 %copy-start.22 = (f32[8,64,8]{1,2,0:T(8,128)S(1)}, f32[8,64,8]{1,2,0:T(8,128)}, u32[]{:S(2)}) copy-start(f32[8,64,8]{1,2,0:T(8,128)} %copy-done.21) | copy-start | bytes 49156
  137.2 258.7 %reduce-scatter.6.cloned.1.call-start = ((), (), s32[]{:S(2)}) async-start(), calls=%async_computation.5 | async-start | bytes 28311552 | tf_op jit(solution)/shard_map/reduce_scatter | solution.py:211
  137.9 3.8 copy-start.10
  198.5 3.2 copy-start.7
  201.8 6.5 %copy-start.3 = (bf16[8,64,8,128]{3,2,1,0:T(8,128)(2,1)S(1)}, bf16[8,64,8,128]{3,2,1,0:T(8,128)(2,1)}, u32[]{:S(2)}) copy-start(bf16[8,64,8,128]{3,2,1,0:T(8,128)(2,1)} %copy-done.2) | copy-start | bytes 3145732
  203.6 43.2 %collective-permute-start = (bf16[512,1024]{1,0:T(8,128)(2,1)}, bf16[512,1024]{1,0:T(8,128)(2,1)S(1)}, u32[]{:S(2)}, u32[]{:S(2)}) collective-permute-start(bf16[512,1024]{1,0:T(8,128)(2,1)} %get-tuple-element.57), channel_id=1, source_target_pairs={{0,1},{1,2},{2,3},{3,0},{4,5},{5,6},{6,7},{7,4},{8,9},{9,10},{10,1... | collective-permute-start | bytes 3145736 | tf_op jit(solution)/shard_map/ppermute | solution.py:115
  205.2 72.1 %collective-permute-start.2 = (bf16[512,1024]{1,0:T(8,128)(2,1)}, bf16[512,1024]{1,0:T(8,128)(2,1)}, u32[]{:S(2)}, u32[]{:S(2)}) collective-permute-start(bf16[512,1024]{1,0:T(8,128)(2,1)} %get-tuple-element.58), channel_id=1, source_target_pairs={{0,3},{1,0},{2,1},{3,2},{4,7},{5,4},{6,5},{7,6},{8,11},{9,8},{10,9... | collective-permute-start | bytes 3145736 | tf_op jit(solution)/shard_map/ppermute | solution.py:115
  207.6 11.3 %slice-start = ((s8[8388608]{0:T(1024)(128)(4,1)}), s8[4194304]{0:T(1024)(128)(4,1)S(1)}, s32[]{:S(2)}) async-start(s8[8388608]{0:T(1024)(128)(4,1)} %bitcast.202), calls=%async_computation.7 | async-start | bytes 8388608
  207.6 11.3 %slice-start.1 = ((s8[8388608]{0:T(1024)(128)(4,1)}), s8[4194304]{0:T(1024)(128)(4,1)S(1)}, s32[]{:S(2)}) async-start(s8[8388608]{0:T(1024)(128)(4,1)} %bitcast.202), calls=%async_computation.8 | async-start | bytes 8388608
  207.6 114.1 %collective-permute-start.1 = (bf16[512,1024]{1,0:T(8,128)(2,1)}, bf16[512,1024]{1,0:T(8,128)(2,1)}, u32[]{:S(2)}, u32[]{:S(2)}) collective-permute-start(bf16[512,1024]{1,0:T(8,128)(2,1)} %get-tuple-element.59), channel_id=1, source_target_pairs={{0,2},{1,3},{2,0},{3,1},{4,6},{5,7},{6,4},{7,5},{8,10},{9,11},{10,... | collective-permute-start | bytes 3145736 | tf_op jit(solution)/shard_map/ppermute | solution.py:115
  242.9 83.5 %collective-permute-start.3 = (bf16[512,1024]{1,0:T(8,128)(2,1)}, bf16[512,1024]{1,0:T(8,128)(2,1)}, u32[]{:S(2)}, u32[]{:S(2)}) collective-permute-start(bf16[512,1024]{1,0:T(8,128)(2,1)} %get-tuple-element.54), channel_id=1, source_target_pairs={{0,1},{1,2},{2,3},{3,0},{4,5},{5,6},{6,7},{7,4},{8,9},{9,10},{10,1... | collective-permute-start | bytes 3145736 | tf_op jit(solution)/shard_map/ppermute | solution.py:115
  244.1 82.3 %collective-permute-start.5 = (bf16[512,1024]{1,0:T(8,128)(2,1)S(1)}, bf16[512,1024]{1,0:T(8,128)(2,1)}, u32[]{:S(2)}, u32[]{:S(2)}) collective-permute-start(bf16[512,1024]{1,0:T(8,128)(2,1)S(1)} %get-tuple-element.55), channel_id=1, source_target_pairs={{0,3},{1,0},{2,1},{3,2},{4,7},{5,4},{6,5},{7,6},{8,11},{9,8},{10,9... | collective-permute-start | bytes 3145736 | tf_op jit(solution)/shard_map/ppermute | solution.py:115
  246.7 140.2 %collective-permute-start.4 = (bf16[512,1024]{1,0:T(8,128)(2,1)S(1)}, bf16[512,1024]{1,0:T(8,128)(2,1)}, u32[]{:S(2)}, u32[]{:S(2)}) collective-permute-start(bf16[512,1024]{1,0:T(8,128)(2,1)S(1)} %get-tuple-element.56), channel_id=1, source_target_pairs={{0,2},{1,3},{2,0},{3,1},{4,6},{5,7},{6,4},{7,5},{8,10},{9,11},{10,... | collective-permute-start | bytes 3145736 | tf_op jit(solution)/shard_map/ppermute | solution.py:115
  277.2 109.7 %copy-start.6 = (bf16[512,1024]{1,0:T(8,128)(2,1)S(1)}, bf16[512,1024]{1,0:T(8,128)(2,1)}, u32[]{:S(2)}) copy-start(bf16[512,1024]{1,0:T(8,128)(2,1)} %param.17) | copy-start | bytes 3145732
  (14 other events, 15.4 us)
Sparse Core Ops, SparseCore 0:
  128.2 33.2 reduce-scatter.3
  165.0 71.2 reduce-scatter.7
  239.9 155.9 reduce-scatter.5
